TPU v7x, 32 devices: a whole 2x2x4 slice. The times are simulated.
32 devices in a mesh: seq: 4 (over y, x), rep: 8 (over z, core).
Axes of the slice: x: 2, y: 2, z: 4, core: 2. Of those that a mesh axis runs over, the one named last changes fastest.
Arguments:
- tile_embed: bfloat16 [8, 4096, 768], P('rep', 'seq'), may hold values from -6 to 6
- tile_source: int32 [8, 4096], P('rep', 'seq'), may hold values from 0 to 4095, as said below
- slide_len: int32 [8], P('rep'), may hold values from 2048 to 4096
- grad_out: bfloat16 [8, 4096, 768], P('rep', 'seq'), may hold values from -6 to 6
- w_query: bfloat16 [768, 768], replicated, may hold values from -0.11727427342914273 to 0.11727427342914273
- w_key: bfloat16 [768, 768], replicated, may hold values from -0.11727427342914273 to 0.11727427342914273
- w_value: bfloat16 [768, 768], replicated, may hold values from -0.21875 to 0.21875
- w_out: bfloat16 [768, 768], replicated, may hold values from -0.21875 to 0.21875
Outputs:
- encoded: bfloat16 [8, 4096, 768], P('rep', 'seq')
- embed_grad: bfloat16 [8, 4096, 768], P('rep', 'seq')
- grad_query: float32 [768, 768], replicated
- grad_key: float32 [768, 768], replicated
- grad_value: float32 [768, 768], replicated
- grad_outproj: float32 [768, 768], replicated
Inputs may be any that keep to these rules, and one draw needn't show every extreme that they name: For each slide, tile_source is a permutation of 0 to 4095; each run of 1024 slide positions (aligned) takes exactly 1024 // (number of such runs) rows from each aligned run of 1024 rows of tile_embed.
All inputs are finite; a program needn't handle non-finite values.
Results may differ from a plain program's by a relative error of at most 0.0025.
The roundings to bfloat16 on the way count: a program that leaves them out, or rounds other values in their place, can miss the bound.
Values may be sent and summed in bfloat16 or wider, within the bound.
No kernel may reach another device: no remote copies, remote signals or barrier semaphores. Data moves between devices by JAX's collectives and lax.ppermute only.
A program may use at most 192 MiB of HBM per device.

v0:
```python
import jax
import jax.numpy as jnp
from jax import lax
from jax.sharding import PartitionSpec as P

HEADS = 16
SEG = 1024
RATE = 16
NEGATIVE = -1e30


def chosen(dilation, head_count):
    return jnp.arange(dilation)[:, None] == (jnp.arange(head_count) % dilation)[None, :]


def sparse_rows(dense, dilation):
    row_count, head_count, trailing = dense.shape
    blocks = dense.astype(jnp.float32).reshape(
        row_count // dilation, dilation, head_count, trailing
    )
    selected = chosen(dilation, head_count)[None, :, :, None]
    return jnp.sum(jnp.where(selected, blocks, jnp.float32(0.0)), axis=1)


def spread_rows(sparse, dilation, filler):
    row_count, head_count, trailing = sparse.shape
    selected = chosen(dilation, head_count)[None, :, :, None]
    spread = jnp.where(selected, sparse[:, None], jnp.float32(filler))
    return spread.reshape(row_count * dilation, head_count, trailing)


def product(pattern, left_side, right_side):
    return jnp.einsum(pattern, left_side, right_side, preferred_element_type=jnp.float32)


def masked_scores(queries, key_rows, key_ok, pieces, scaling):
    scores = product("nqd,nkd->nqk", queries, key_rows) * scaling
    return jnp.where(key_ok.reshape(pieces, 1, -1), scores, NEGATIVE)


def head_forward(queries, key_rows, values, key_ok, pieces, scaling):
    head_width = queries.shape[-1]
    queries = queries.reshape(pieces, -1, head_width)
    key_rows = key_rows.reshape(pieces, -1, head_width)
    values = values.reshape(pieces, -1, head_width)
    scores = masked_scores(queries, key_rows, key_ok, pieces, scaling)
    maxima = jnp.max(scores, axis=-1)
    weights = jnp.exp(scores - maxima[..., None])
    totals = jnp.sum(weights, axis=-1)
    numerator = product("nqk,nkd->nqd", weights.astype(jnp.bfloat16), values)
    return (numerator.reshape(-1, head_width), maxima.reshape(-1), totals.reshape(-1))


def split_pieces(arrays, pieces):
    return tuple((member.reshape(pieces, -1, member.shape[-1]) for member in arrays))


def score_terms(queries, key_rows, values, key_ok, log_total, upstream, deltas, pieces, scaling):
    scores = masked_scores(queries, key_rows, key_ok, pieces, scaling)
    probabilities = jnp.exp(scores - log_total.reshape(pieces, -1, 1))
    prob_grad = product("nqd,nkd->nqk", upstream, values)
    score_grad = (probabilities * (prob_grad - deltas.reshape(pieces, -1, 1))).astype(jnp.bfloat16)
    return (probabilities, score_grad)


def head_backward(queries, key_rows, values, key_ok, log_total, upstream, deltas, pieces, scaling):
    head_width = queries.shape[-1]
    queries, key_rows, values, upstream = split_pieces(
        (queries, key_rows, values, upstream), pieces
    )
    probabilities, score_grad = score_terms(
        queries, key_rows, values, key_ok, log_total, upstream, deltas, pieces, scaling
    )
    value_grad = product("nqk,nqd->nkd", probabilities.astype(jnp.bfloat16), upstream)
    query_grad = product("nqk,nkd->nqd", score_grad, key_rows) * scaling
    key_grad = product("nqk,nqd->nkd", score_grad, queries) * scaling
    return (
        query_grad.reshape(-1, head_width),
        key_grad.reshape(-1, head_width),
        value_grad.reshape(-1, head_width),
    )


def heads_map(function, arrays, pieces, scaling):
    transposed = tuple((jnp.moveaxis(member, 1, 0) for member in arrays))
    results = lax.map(lambda members: function(*members, pieces, scaling), transposed)
    return tuple((jnp.moveaxis(member, 0, 1) for member in results))


def merge_parts(local_part, remote, dilation):
    numer_local, max_local, total_local = local_part
    numer_far = spread_rows(remote[0], dilation, 0.0)
    max_far = spread_rows(remote[1][..., None], dilation, NEGATIVE)[..., 0]
    total_far = spread_rows(remote[2][..., None], dilation, 0.0)[..., 0]
    highest = jnp.maximum(max_local, max_far)
    weight_local = jnp.exp(max_local - highest)
    weight_far = jnp.exp(max_far - highest)
    combined = total_local * weight_local + total_far * weight_far
    output = (numer_local * weight_local[..., None] + numer_far * weight_far[..., None]) / combined[
        ..., None
    ]
    return (output, highest + jnp.log(combined))


def project(left_side, right_side):
    return jnp.dot(left_side, right_side, preferred_element_type=jnp.float32)


def per_device(tile_embed, tile_source, slide_len, grad_out, w_query, w_key, w_value, w_out):
    owned_rows = tile_embed[0]
    source = tile_source[0]
    row_count, features = owned_rows.shape
    stripes = lax.axis_size("seq")
    stripe = lax.axis_index("seq")
    portion = row_count // stripes
    owner_dev = source // row_count
    ordering = jnp.argsort(owner_dev, stable=True)
    wanted = (source % row_count)[ordering].reshape(stripes, portion)
    requested = lax.all_to_all(wanted, "seq", split_axis=0, concat_axis=0, tiled=True)
    picked = jnp.take(owned_rows, requested.reshape(-1), axis=0).reshape(stripes, portion, features)
    arrived = lax.all_to_all(picked, "seq", split_axis=0, concat_axis=0, tiled=True).reshape(
        row_count, features
    )
    embedded = jnp.zeros_like(arrived).at[ordering].set(arrived)
    length = slide_len[0]
    upstream_in = grad_out[0]
    head_dim = features // HEADS
    scaling = head_dim ** (-0.5)
    positions = stripe * row_count + jnp.arange(row_count)
    valid_rows = positions < length
    queries = project(embedded, w_query).astype(jnp.bfloat16).reshape(row_count, HEADS, head_dim)
    key_rows = project(embedded, w_key).astype(jnp.bfloat16).reshape(row_count, HEADS, head_dim)
    values = project(embedded, w_value).astype(jnp.bfloat16).reshape(row_count, HEADS, head_dim)
    local_ok = jnp.broadcast_to(valid_rows[:, None], (row_count, HEADS))
    local_part = heads_map(
        head_forward, (queries, key_rows, values, local_ok), row_count // SEG, scaling
    )
    sparse_q = sparse_rows(queries, RATE).astype(jnp.bfloat16)
    sparse_k = sparse_rows(key_rows, RATE).astype(jnp.bfloat16)
    sparse_v = sparse_rows(values, RATE).astype(jnp.bfloat16)
    near_count = sparse_k.shape[0]
    far_k, far_v = (
        lax.all_gather(sparse_k.reshape(near_count, features), "seq", axis=0, tiled=True),
        lax.all_gather(sparse_v.reshape(near_count, features), "seq", axis=0, tiled=True),
    )
    far_count = far_k.shape[0]
    far_k = far_k.reshape(far_count, HEADS, head_dim)
    far_v = far_v.reshape(far_count, HEADS, head_dim)
    sparse_pos = jnp.arange(far_count)[:, None] * RATE + (jnp.arange(HEADS) % RATE)[None, :]
    sparse_ok = sparse_pos < length
    remote = heads_map(head_forward, (sparse_q, far_k, far_v, sparse_ok), 1, scaling)
    output, log_total = merge_parts(local_part, remote, RATE)
    attended = (
        (output * valid_rows[:, None, None]).astype(jnp.bfloat16).reshape(row_count, features)
    )
    encoded = (embedded.astype(jnp.float32) + project(attended, w_out)).astype(jnp.bfloat16)
    upstream = (
        (project(upstream_in, w_out.T) * valid_rows[:, None])
        .astype(jnp.bfloat16)
        .reshape(row_count, HEADS, head_dim)
    )
    deltas = jnp.sum(upstream.astype(jnp.float32) * output, axis=-1)
    grad_outproj = jnp.einsum(
        "td,te->de", attended, upstream_in, preferred_element_type=jnp.float32
    )
    local_grads = heads_map(
        head_backward,
        (queries, key_rows, values, local_ok, log_total, upstream, deltas),
        row_count // SEG,
        scaling,
    )
    sparse_up = sparse_rows(upstream, RATE).astype(jnp.bfloat16)
    sparse_delta = sparse_rows(deltas[..., None], RATE)[..., 0]
    sparse_total = sparse_rows(log_total[..., None], RATE)[..., 0]
    remote_grads = heads_map(
        head_backward,
        (sparse_q, far_k, far_v, sparse_ok, sparse_total, sparse_up, sparse_delta),
        1,
        scaling,
    )
    key_back, value_back = (
        lax.psum_scatter(
            remote_grads[1].reshape(far_count, features), "seq", scatter_dimension=0, tiled=True
        ),
        lax.psum_scatter(
            remote_grads[2].reshape(far_count, features), "seq", scatter_dimension=0, tiled=True
        ),
    )
    key_back = key_back.reshape(near_count, HEADS, head_dim)
    value_back = value_back.reshape(near_count, HEADS, head_dim)
    query_far = remote_grads[0]
    query_grad = (
        (local_grads[0] + spread_rows(query_far, RATE, 0.0))
        .astype(jnp.bfloat16)
        .reshape(row_count, features)
    )
    key_grad = (
        (local_grads[1] + spread_rows(key_back, RATE, 0.0))
        .astype(jnp.bfloat16)
        .reshape(row_count, features)
    )
    value_grad = (
        (local_grads[2] + spread_rows(value_back, RATE, 0.0))
        .astype(jnp.bfloat16)
        .reshape(row_count, features)
    )
    embed_grad = upstream_in.astype(jnp.float32) + project(query_grad, w_query.T)
    embed_grad = embed_grad + project(key_grad, w_key.T)
    embed_grad = (embed_grad + project(value_grad, w_value.T)).astype(jnp.bfloat16)
    grad_query = jnp.einsum("td,te->de", embedded, query_grad, preferred_element_type=jnp.float32)
    grad_key = jnp.einsum("td,te->de", embedded, key_grad, preferred_element_type=jnp.float32)
    grad_value = jnp.einsum("td,te->de", embedded, value_grad, preferred_element_type=jnp.float32)
    summed = lax.psum((grad_query, grad_key, grad_value, grad_outproj), ("seq", "rep"))
    return (encoded[None], embed_grad[None], summed[0], summed[1], summed[2], summed[3])


def solution(mesh):
    return jax.shard_map(
        per_device,
        mesh=mesh,
        in_specs=(
            P("rep", "seq", None),
            P("rep", "seq"),
            P("rep"),
            P("rep", "seq", None),
            P(),
            P(),
            P(),
            P(),
        ),
        out_specs=(P("rep", "seq", None), P("rep", "seq", None), P(), P(), P(), P()),
        check_vma=False,
    )
```

profile of v0, /device:TPU:0, one launch (start us, length us, event | category | flops | bytes accessed | tf_op | source)
XLA Modules:
  0.0 939.3 jit_solution(3229480369411910893)
XLA Ops:
  8.0 4.4 sort.17
  12.4 4.5 gather_fusion
  16.9 9.7 %all_to_all.14 = s32[4,1,256]{2,1,0:T(1,128)S(1)} all-to-all(s32[4,1,256]{2,1,0:T(1,128)S(1)} %bitcast.389), channel_id=1, replica_groups=mesh['seq'=4,'rep'=8] {'seq'}, dimensions={0} | all-to-all | bytes 8192 | tf_op jit(solution)/shard_map/all_to_all | solution.py:119
  32.0 4.5 all-to-all-start.1
  43.2 7.8 reshape.434
  53.0 4.9 copy.100
  58.0 6.4 scatter_custom_fusion
  69.7 7.8 reshape.431
  82.9 7.8 reshape.432
  90.7 4.3 convolution_convert_fusion
  98.1 7.8 reshape.433
  105.9 14.5 %select_reduce_fusion = (bf16[64,16,48]{2,1,0:T(8,128)(2,1)}, bf16[64,16,48]{2,1,0:T(8,128)(2,1)S(1)}, bf16[64,16,48]{2,1,0:T(8,128)(2,1)S(1)}, bf16[64,16,48]{2,1,0:T(8,128)(2,1)}) fusion(f32[64,16,16,48]{3,2,1,0:T(8,128)} %reshape.434, pred[16,16]{1,0:T(8,128)(4,1)S(1)} %iota_compare_fusion, f32[64,16,16,48]{3,2,1,0:T(8,128)} %reshape.432, ...), kind=kLoop, calls=%fused_computation.133 | loop fusion | flops 6094848 | bytes 12976384 | tf_op jit(solution)/shard_map/reduce_sum | solution.py:22
  120.6 10.6 %all_gather.6 = bf16[256,768]{1,0:T(8,128)(2,1)S(1)} all-gather(bf16[64,768]{1,0:T(8,128)(2,1)S(1)} %convert_element_type.144), channel_id=1, replica_groups=mesh['seq'=4,'rep'=8] {'seq'}, dimensions={0}, use_global_device_ids=true | all-gather | bytes 491520 | tf_op jit(solution)/shard_map/all_gather | solution.py:143
  132.2 8.9 all_gather.7
  143.7 26.0 %while.57 = (s32[]{:T(128)}, f32[16,64,48]{1,2,0:T(8,128)S(1)}, f32[16,64]{1,0:T(8,128)S(1)}, f32[16,64]{1,0:T(8,128)S(1)}, pred[16,256]{1,0:T(8,128)(4,1)S(1)},...) while((s32[]{:T(128)}, f32[16,64,48]{1,2,0:T(8,128)S(1)}, ...), condition=%wide.region_12.13_spmd, body=%wide.region_9.12_spmd.sunk | while | flops 3260290 | bytes 374129 | solution.py:86
  187.5 142.6 %while.56 = (s32[]{:T(128)}, f32[16,1024,48]{1,2,0:T(8,128)}, f32[16,1024]{1,0:T(8,128)S(1)}, f32[16,1024]{1,0:T(8,128)S(1)}, pred[16,1024]{1,0:T(8,128)(4,1)S(1...) while((s32[]{:T(128)}, f32[16,1024,48]{1,2,0:T(8,128)}, ...), condition=%wide.region_5.6_spmd, body=%wide.region_2.5_spmd.sunk | while | flops 212858880 | bytes 30383244 | solution.py:86
  332.5 7.9 copy.83
  340.4 13.4 %multiply_convert_fusion.1 = (bf16[1024,16,48]{2,1,0:T(8,128)(2,1)}, f32[1024,16,48]{2,1,0:T(8,128)S(1)}) fusion(f32[1024]{0:T(1024)S(1)} %copy-done.34, f32[1024,16]{1,0:T(8,128)} %copy.97, f32[1024,16]{1,0:T(8,128)S(1)} %copy.96, f32[64,16,48]{2,1,0:T(8,128)S(1)} %copy.95, pred[1024,16]{1,0:T(8,128)(4,1)S(1)} %copy-done.19, f32[1024,16]{1,0:T(8,128)S(1)} %copy.93, ...), kind=kLoop, calls=%fused_computation.135 | loop fusion | flops 5505024 | bytes 8278016 | tf_op jit(solution)/shard_map/convert_element_type | solution.py:154
  357.3 98.4 %while.59 = (s32[]{:T(128)}, f32[16,64,48]{1,2,0:T(8,128)S(1)}, f32[16,256,48]{1,2,0:T(8,128)}, f32[16,256,48]{1,2,0:T(8,128)}, pred[16,256]{1,0:T(8,128)(4,1)},...) while((s32[]{:T(128)}, f32[16,64,48]{1,2,0:T(8,128)S(1)}, ...), condition=%wide.region_20.21_spmd, body=%wide.region_19.20_spmd.sunk | while | flops 7994370 | bytes 687741 | solution.py:86
  470.3 181.2 %while.58 = (s32[]{:T(128)}, f32[16,1024,48]{1,2,0:T(8,128)}, f32[16,1024,48]{1,2,0:T(8,128)}, f32[16,1024,48]{1,2,0:T(8,128)}, pred[16,1024]{1,0:T(8,128)(4,1)S...) while((s32[]{:T(128)}, f32[16,1024,48]{1,2,0:T(8,128)}, ...), condition=%wide.region_15.16_spmd, body=%wide.region_14.15_spmd.sunk | while | flops 513900544 | bytes 21337212 | solution.py:86
  651.8 7.9 copy.102
  659.6 7.8 copy.112
  667.5 7.9 copy.115
  675.3 5.5 copy.98
  687.8 15.2 %fusion.110 = (bf16[1024,16,48]{2,1,0:T(8,128)(2,1)}, bf16[1024,16,48]{2,1,0:T(8,128)(2,1)}, bf16[1024,16,48]{2,1,0:T(8,128)(2,1)}) fusion(f32[16,1024,48]{2,0,1:T(8,128)} %copy.102, f32[64,16,48]{2,1,0:T(8,128)S(1)} %copy.110, pred[1024,16]{1,0:T(8,128)(4,1)} %copy.94, f32[64,16,48]{2,1,0:T(8,128)S(1)} %copy.113, f32[16,1024,48]{2,0,1:T(8,128)} %copy.112, ...), kind=kLoop, calls=%fused_computation.127 | loop fusion | flops 7077888 | bytes 14761984 | tf_op jit(solution)/shard_map/convert_element_type | solution.py:194
  703.0 5.5 copy.111
  712.7 5.5 copy.114
  718.2 4.2 fusion.131
  722.5 4.4 copy.117
  727.0 4.2 fusion.132
  731.2 5.0 fusion.117
  742.9 179.8 %all-reduce.3.cloned.1.call-done = (f32[768,768]{1,0:T(8,128)}, f32[768,768]{1,0:T(8,128)}, f32[768,768]{1,0:T(8,128)}, f32[768,768]{1,0:T(8,128)}) async-done(((f32[768,768]{1,0:T(8,128)}, f32[768,768]{1,0:T(8,128)}, f32[768,768]{1,0:T(8,128)}, f32[768,768]{1,0:T(8,128)}), (f32[768,768]{1,0:T(8,128)}, f32[768,768]{1,0:T(8,128)}, f32[768,768]{1,0:T(8,128)}, ...) | async-done | bytes 9437200 | tf_op jit(solution)/shard_map/psum | solution.py:213
  (612 shorter events, 543.6 us)
Async XLA Ops:
  7.2 19.4 %copy-start = (bf16[1,1024,768]{2,1,0:T(8,128)(2,1)S(1)}, bf16[1,1024,768]{2,1,0:T(8,128)(2,1)}, u32[]{:S(2)}) copy-start(bf16[1,1024,768]{2,1,0:T(8,128)(2,1)} %param.16) | copy-start | bytes 4718596
  32.0 6.3 copy-start.13
  32.0 26.0 %all-to-all-start.1 = ((bf16[4,256,768]{2,1,0:T(8,128)(2,1)}), bf16[4,256,768]{2,1,0:T(8,128)(2,1)}, u32[]{:S(2)}, u32[]{:S(2)}) async-start(bf16[4,256,768]{2,1,0:T(8,128)(2,1)} %broadcast_select_fusion), calls=%async_computation.1 | async-start | bytes 3145728 | tf_op jit(solution)/shard_map/all_to_all | solution.py:121
  36.5 648.5 %reduce-scatter.7.cloned.1.call-start = ((), (), s32[]{:S(2)}) async-start(), calls=%async_computation.4 | async-start | bytes 983040
  41.0 12.0 %copy-start.4 = (bf16[1024,768]{0,1:T(8,128)(2,1)}, bf16[1024,768]{0,1:T(8,128)(2,1)S(1)}, u32[]{:S(2)}) copy-start(bf16[1024,768]{0,1:T(8,128)(2,1)S(1)} %multiply_convert_fusion.2) | copy-start | bytes 4718596
  52.1 5.8 copy-start.26
  64.4 3.3 copy-start.15
  80.7 10.1 %copy-start.6 = (bf16[1024,768]{0,1:T(8,128)(2,1)}, bf16[1024,768]{0,1:T(8,128)(2,1)S(1)}, u32[]{:S(2)}) copy-start(bf16[1024,768]{0,1:T(8,128)(2,1)S(1)} %convolution_convert_fusion.1) | copy-start | bytes 4718596
  131.2 12.4 %copy-start.35 = (f32[16,64]{1,0:T(8,128)S(1)}, f32[16,64]{1,0:T(8,128)}, u32[]{:S(2)}) copy-start(f32[16,64]{1,0:T(8,128)} %custom-call.7) | copy-start | bytes 12292
  169.6 3.2 copy-start.9
  169.6 3.2 copy-start.22
  169.7 9.4 copy-start.30
  173.8 5.2 copy-start.7
  179.0 3.2 copy-start.8
  182.2 3.2 copy-start.36
  182.2 5.2 copy-start.28
  182.2 5.2 copy-start.29
  187.5 142.6 %copy-start.24 = (f32[1024,16]{0,1:T(8,128)S(1)}, f32[1024,16]{0,1:T(8,128)}, u32[]{:S(2)}) copy-start(f32[1024,16]{0,1:T(8,128)} %broadcast_in_dim.318) | copy-start | bytes 196612
  187.5 142.6 %copy-start.25 = (f32[1024,16]{0,1:T(8,128)S(1)}, f32[1024,16]{0,1:T(8,128)}, u32[]{:S(2)}) copy-start(f32[1024,16]{0,1:T(8,128)} %broadcast_in_dim.325) | copy-start | bytes 196612
  187.5 142.6 %copy-start.27 = (pred[1024,16]{0,1:T(8,128)(4,1)S(1)}, pred[1024,16]{0,1:T(8,128)(4,1)}, u32[]{:S(2)}) copy-start(pred[1024,16]{0,1:T(8,128)(4,1)} %copy-done.26) | copy-start | bytes 49156
  332.5 7.9 copy-start.19
  332.5 7.9 copy-start.34
  340.4 13.4 %copy-start.3 = (bf16[1024,16,48]{2,1,0:T(8,128)(2,1)S(1)}, bf16[1024,16,48]{2,1,0:T(8,128)(2,1)}, u32[]{:S(2)}) copy-start(bf16[1024,16,48]{2,1,0:T(8,128)(2,1)} %copy.100) | copy-start | bytes 4718596
  357.2 100.8 %copy-start.5 = (bf16[1024,768]{0,1:T(8,128)(2,1)S(1)}, bf16[1024,768]{0,1:T(8,128)(2,1)}, u32[]{:S(2)}) copy-start(bf16[1024,768]{0,1:T(8,128)(2,1)} %copy-done.4) | copy-start | bytes 4718596
  458.0 228.4 %reduce-scatter.9.cloned.1.call-start = ((), (), s32[]{:S(2)}) async-start(), calls=%async_computation.5 | async-start | bytes 983040
  463.7 459.1 %all-reduce.3.cloned.1.call-start = ((), (), s32[]{:S(2)}) async-start(), calls=%async_computation.6 | async-start | bytes 18874368 | tf_op jit(solution)/shard_map/psum | solution.py:213
  675.3 5.5 copy-start.14
  703.0 5.5 copy-start.16
  731.2 5.0 copy-start.17
  731.2 5.0 copy-start.37
  922.7 3.4 copy-start.12
  928.6 3.9 copy-start.1
  (26 other events, 51.9 us)
Sparse Core Ops, SparseCore 0:
  458.1 26.4 reduce-scatter.6
  488.0 26.1 reduce-scatter.8
  731.3 191.3 all-reduce.2
where the time goes:
time: 954 us; the launch traced here: 939 us
  matrix products  421 us (44%)
  local copies, waits for them, and re-layouts  215 us (23%)
  waiting for transfers between devices  180 us (19%)
  other arithmetic  71.3 us (7%)
  blocking collectives  29.2 us (3%)
  between operations  15.2 us (2%)
    dot_general x224, matrix products, product(): jnp.einsum(pattern, left_side, right_side, preferred_element_type=jnp.flo...  380 us
    psum x1, waiting for transfers between devices, per_device(): lax.psum((grad_query, grad_key, grad_value, grad_outproj), ('seq', 'rep'))  180 us
    while x9, local copies, waits for them, and re-layouts, heads_map(): lax.map(lambda members: function(*members, pieces, scaling), transposed)  34.5 us
    while x32, local copies, waits for them, and re-layouts  30.9 us
    convert_element_type x6, local copies, waits for them, and re-layouts, sparse_rows(): dense.astype(jnp.float32)  30.7 us
    dot_general x8, matrix products, project(): return jnp.dot(left_side, right_side, preferred_element_type=jnp.float32)  24 us
  transfers between devices with their start and end apart: 4, of which 1 were waited for; matrix products, arithmetic and copies ran while one was open for 27% of the time, Pallas kernels for 0%

commit v1 on v0

--- a/solution.py
+++ b/solution.py
@@ -2,6 +2,7 @@
 import jax.numpy as jnp
 from jax import lax
 from jax.sharding import PartitionSpec as P
+from jax.lax import psum
 
 HEADS = 16
 SEG = 1024
@@ -210,7 +211,7 @@
     grad_query = jnp.einsum("td,te->de", embedded, query_grad, preferred_element_type=jnp.float32)
     grad_key = jnp.einsum("td,te->de", embedded, key_grad, preferred_element_type=jnp.float32)
     grad_value = jnp.einsum("td,te->de", embedded, value_grad, preferred_element_type=jnp.float32)
-    summed = lax.psum((grad_query, grad_key, grad_value, grad_outproj), ("seq", "rep"))
+    summed = psum(psum((grad_query, grad_key, grad_value, grad_outproj), "seq"), "rep")
     return (encoded[None], embed_grad[None], summed[0], summed[1], summed[2], summed[3])
 
 

time: 954 us -> 1150 us (1.21)
  waiting for transfers between devices: 180 us -> 376 us
    psum x1 -> x2, waiting for transfers between devices: 180 us -> 376 us  [the longest x1 189 us: per_device(): psum((grad_query, grad_key, grad_value, grad_outproj), 'seq')]
  transfers between devices with their start and end apart: 4 -> 5, of which waited for: 1 -> 2; matrix products, arithmetic and copies ran while one was open for 27% -> 23% of each run, Pallas kernels for 0% -> 0%
where the time goes in v1:
time: 1150 us; the launch traced here: 1130 us
  matrix products  421 us (37%)
  waiting for transfers between devices  376 us (33%)
  local copies, waits for them, and re-layouts  215 us (19%)
  other arithmetic  71.3 us (6%)
  blocking collectives  29.2 us (3%)
  between operations  15.2 us (1%)
    dot_general x224, matrix products, product(): jnp.einsum(pattern, left_side, right_side, preferred_element_type=jnp.flo...  380 us
    psum x1, waiting for transfers between devices, per_device(): psum((grad_query, grad_key, grad_value, grad_outproj), 'seq')  189 us
    psum x1, waiting for transfers between devices, per_device(): psum(psum((grad_query, grad_key, grad_value, grad_outproj), 'seq'), 'rep')  187 us
    while x9, local copies, waits for them, and re-layouts, heads_map(): lax.map(lambda members: function(*members, pieces, scaling), transposed)  34.5 us
    while x32, local copies, waits for them, and re-layouts  31 us
    convert_element_type x6, local copies, waits for them, and re-layouts, sparse_rows(): dense.astype(jnp.float32)  30.7 us
    dot_general x8, matrix products, project(): return jnp.dot(left_side, right_side, preferred_element_type=jnp.float32)  24 us
  transfers between devices with their start and end apart: 5, of which 2 were waited for; matrix products, arithmetic and copies ran while one was open for 23% of the time, Pallas kernels for 0%

profile of v1, /device:TPU:0, one launch (start us, length us, event | category | flops | bytes accessed | tf_op | source)
XLA Modules:
  0.0 1134.9 jit_solution(1358193090605964865)
XLA Ops:
  8.0 4.4 sort.17
  12.4 4.5 gather_fusion
  16.9 9.7 all_to_all.14
  32.0 4.5 all-to-all-start.1
  43.4 7.8 reshape.434
  53.2 4.9 copy.100
  58.1 6.4 scatter_custom_fusion
  69.9 7.8 reshape.431
  83.0 7.8 reshape.432
  90.9 4.3 convolution_convert_fusion
  98.2 7.8 reshape.433
  106.0 14.5 %select_reduce_fusion = (bf16[64,16,48]{2,1,0:T(8,128)(2,1)}, bf16[64,16,48]{2,1,0:T(8,128)(2,1)S(1)}, bf16[64,16,48]{2,1,0:T(8,128)(2,1)S(1)}, bf16[64,16,48]{2,1,0:T(8,128)(2,1)}) fusion(f32[64,16,16,48]{3,2,1,0:T(8,128)} %reshape.434, pred[16,16]{1,0:T(8,128)(4,1)S(1)} %iota_compare_fusion, f32[64,16,16,48]{3,2,1,0:T(8,128)} %reshape.432, ...), kind=kLoop, calls=%fused_computation.133 | loop fusion | flops 6094848 | bytes 12976384 | tf_op jit(solution)/shard_map/reduce_sum | solution.py:23
  120.7 10.6 all_gather.6
  132.3 8.9 all_gather.7
  143.8 26.0 %while.57 = (s32[]{:T(128)}, f32[16,64,48]{1,2,0:T(8,128)S(1)}, f32[16,64]{1,0:T(8,128)S(1)}, f32[16,64]{1,0:T(8,128)S(1)}, pred[16,256]{1,0:T(8,128)(4,1)S(1)},...) while((s32[]{:T(128)}, f32[16,64,48]{1,2,0:T(8,128)S(1)}, ...), condition=%wide.region_12.13_spmd, body=%wide.region_9.12_spmd.sunk | while | flops 3260290 | bytes 374129 | solution.py:87
  187.6 142.7 %while.56 = (s32[]{:T(128)}, f32[16,1024,48]{1,2,0:T(8,128)}, f32[16,1024]{1,0:T(8,128)S(1)}, f32[16,1024]{1,0:T(8,128)S(1)}, pred[16,1024]{1,0:T(8,128)(4,1)S(1...) while((s32[]{:T(128)}, f32[16,1024,48]{1,2,0:T(8,128)}, ...), condition=%wide.region_5.6_spmd, body=%wide.region_2.5_spmd.sunk | while | flops 212858880 | bytes 30383244 | solution.py:87
  332.8 7.9 copy.83
  340.7 13.4 %multiply_convert_fusion.1 = (bf16[1024,16,48]{2,1,0:T(8,128)(2,1)}, f32[1024,16,48]{2,1,0:T(8,128)S(1)}) fusion(f32[1024]{0:T(1024)S(1)} %copy-done.34, f32[1024,16]{1,0:T(8,128)} %copy.97, f32[1024,16]{1,0:T(8,128)S(1)} %copy.96, f32[64,16,48]{2,1,0:T(8,128)S(1)} %copy.95, pred[1024,16]{1,0:T(8,128)(4,1)S(1)} %copy-done.19, f32[1024,16]{1,0:T(8,128)S(1)} %copy.93, ...), kind=kLoop, calls=%fused_computation.135 | loop fusion | flops 5505024 | bytes 8278016 | tf_op jit(solution)/shard_map/convert_element_type | solution.py:155
  357.5 98.4 %while.59 = (s32[]{:T(128)}, f32[16,64,48]{1,2,0:T(8,128)S(1)}, f32[16,256,48]{1,2,0:T(8,128)}, f32[16,256,48]{1,2,0:T(8,128)}, pred[16,256]{1,0:T(8,128)(4,1)},...) while((s32[]{:T(128)}, f32[16,64,48]{1,2,0:T(8,128)S(1)}, ...), condition=%wide.region_20.21_spmd, body=%wide.region_19.20_spmd.sunk | while | flops 7994370 | bytes 687741 | solution.py:87
  470.6 181.2 %while.58 = (s32[]{:T(128)}, f32[16,1024,48]{1,2,0:T(8,128)}, f32[16,1024,48]{1,2,0:T(8,128)}, f32[16,1024,48]{1,2,0:T(8,128)}, pred[16,1024]{1,0:T(8,128)(4,1)S...) while((s32[]{:T(128)}, f32[16,1024,48]{1,2,0:T(8,128)}, ...), condition=%wide.region_15.16_spmd, body=%wide.region_14.15_spmd.sunk | while | flops 513900544 | bytes 21337212 | solution.py:87
  652.1 7.9 copy.102
  660.0 7.8 copy.112
  667.8 7.9 copy.115
  675.7 5.5 copy.98
  688.2 15.2 %fusion.110 = (bf16[1024,16,48]{2,1,0:T(8,128)(2,1)}, bf16[1024,16,48]{2,1,0:T(8,128)(2,1)}, bf16[1024,16,48]{2,1,0:T(8,128)(2,1)}) fusion(f32[16,1024,48]{2,0,1:T(8,128)} %copy.102, f32[64,16,48]{2,1,0:T(8,128)S(1)} %copy.110, pred[1024,16]{1,0:T(8,128)(4,1)} %copy.94, f32[64,16,48]{2,1,0:T(8,128)S(1)} %copy.113, f32[16,1024,48]{2,0,1:T(8,128)} %copy.112, ...), kind=kLoop, calls=%fused_computation.127 | loop fusion | flops 7077888 | bytes 14761984 | tf_op jit(solution)/shard_map/convert_element_type | solution.py:195
  703.4 5.5 copy.111
  713.1 5.5 copy.114
  722.8 4.4 copy.117
  727.3 4.2 fusion.132
  731.6 188.9 %all-reduce.7.cloned.1.call-done = (f32[768,768]{1,0:T(8,128)}, f32[768,768]{1,0:T(8,128)}, f32[768,768]{1,0:T(8,128)}, f32[768,768]{1,0:T(8,128)}) async-done(((f32[768,768]{1,0:T(8,128)}, f32[768,768]{1,0:T(8,128)}, f32[768,768]{1,0:T(8,128)}, f32[768,768]{1,0:T(8,128)}), (f32[768,768]{1,0:T(8,128)}, f32[768,768]{1,0:T(8,128)}, f32[768,768]{1,0:T(8,128)}, ...) | async-done | bytes 9437200 | tf_op jit(solution)/shard_map/psum | solution.py:214
  920.5 5.0 fusion.117
  931.4 186.9 %all-reduce.5.cloned.1.call-done = (f32[768,768]{1,0:T(8,128)}, f32[768,768]{1,0:T(8,128)}, f32[768,768]{1,0:T(8,128)}, f32[768,768]{1,0:T(8,128)}) async-done(((f32[768,768]{1,0:T(8,128)}, f32[768,768]{1,0:T(8,128)}, f32[768,768]{1,0:T(8,128)}, f32[768,768]{1,0:T(8,128)}), (f32[768,768]{1,0:T(8,128)}, f32[768,768]{1,0:T(8,128)}, f32[768,768]{1,0:T(8,128)}, ...) | async-done | bytes 9437200 | tf_op jit(solution)/shard_map/psum | solution.py:214
  (615 shorter events, 547.4 us)
Async XLA Ops:
  7.2 19.4 %copy-start = (bf16[1,1024,768]{2,1,0:T(8,128)(2,1)S(1)}, bf16[1,1024,768]{2,1,0:T(8,128)(2,1)}, u32[]{:S(2)}) copy-start(bf16[1,1024,768]{2,1,0:T(8,128)(2,1)} %param.16) | copy-start | bytes 4718596
  32.0 6.4 copy-start.13
  32.0 26.1 %all-to-all-start.1 = ((bf16[4,256,768]{2,1,0:T(8,128)(2,1)}), bf16[4,256,768]{2,1,0:T(8,128)(2,1)}, u32[]{:S(2)}, u32[]{:S(2)}) async-start(bf16[4,256,768]{2,1,0:T(8,128)(2,1)} %broadcast_select_fusion), calls=%async_computation.1 | async-start | bytes 3145728 | tf_op jit(solution)/shard_map/all_to_all | solution.py:122
  36.5 648.9 %reduce-scatter.7.cloned.1.call-start = ((), (), s32[]{:S(2)}) async-start(), calls=%async_computation.4 | async-start | bytes 983040
  41.1 12.0 %copy-start.4 = (bf16[1024,768]{0,1:T(8,128)(2,1)}, bf16[1024,768]{0,1:T(8,128)(2,1)S(1)}, u32[]{:S(2)}) copy-start(bf16[1024,768]{0,1:T(8,128)(2,1)S(1)} %multiply_convert_fusion.2) | copy-start | bytes 4718596
  52.3 5.8 copy-start.26
  64.5 3.3 copy-start.15
  80.8 10.0 copy-start.6
  131.4 12.4 %copy-start.35 = (f32[16,64]{1,0:T(8,128)S(1)}, f32[16,64]{1,0:T(8,128)}, u32[]{:S(2)}) copy-start(f32[16,64]{1,0:T(8,128)} %custom-call.7) | copy-start | bytes 12292
  169.8 3.2 copy-start.9
  169.8 9.4 copy-start.30
  173.9 5.2 copy-start.7
  179.2 3.2 copy-start.8
  182.4 3.2 copy-start.36
  182.4 5.3 copy-start.28
  182.4 5.3 copy-start.29
  187.6 142.7 %copy-start.24 = (f32[1024,16]{0,1:T(8,128)S(1)}, f32[1024,16]{0,1:T(8,128)}, u32[]{:S(2)}) copy-start(f32[1024,16]{0,1:T(8,128)} %broadcast_in_dim.318) | copy-start | bytes 196612
  187.6 142.7 %copy-start.25 = (f32[1024,16]{0,1:T(8,128)S(1)}, f32[1024,16]{0,1:T(8,128)}, u32[]{:S(2)}) copy-start(f32[1024,16]{0,1:T(8,128)} %broadcast_in_dim.325) | copy-start | bytes 196612
  187.6 142.7 %copy-start.27 = (pred[1024,16]{0,1:T(8,128)(4,1)S(1)}, pred[1024,16]{0,1:T(8,128)(4,1)}, u32[]{:S(2)}) copy-start(pred[1024,16]{0,1:T(8,128)(4,1)} %copy-done.26) | copy-start | bytes 49156
  332.7 7.9 copy-start.19
  332.7 7.9 copy-start.34
  340.7 13.4 %copy-start.3 = (bf16[1024,16,48]{2,1,0:T(8,128)(2,1)S(1)}, bf16[1024,16,48]{2,1,0:T(8,128)(2,1)}, u32[]{:S(2)}) copy-start(bf16[1024,16,48]{2,1,0:T(8,128)(2,1)} %copy.100) | copy-start | bytes 4718596
  357.5 100.8 %copy-start.5 = (bf16[1024,768]{0,1:T(8,128)(2,1)S(1)}, bf16[1024,768]{0,1:T(8,128)(2,1)}, u32[]{:S(2)}) copy-start(bf16[1024,768]{0,1:T(8,128)(2,1)} %copy-done.4) | copy-start | bytes 4718596
  458.2 228.5 %reduce-scatter.9.cloned.1.call-start = ((), (), s32[]{:S(2)}) async-start(), calls=%async_computation.5 | async-start | bytes 983040
  463.9 456.6 %all-reduce.7.cloned.1.call-start = ((), (), s32[]{:S(2)}) async-start(), calls=%async_computation.7 | async-start | bytes 18874368 | tf_op jit(solution)/shard_map/psum | solution.py:214
  675.7 5.5 copy-start.14
  703.3 5.5 copy-start.16
  731.6 386.8 %all-reduce.5.cloned.1.call-start = ((), (), s32[]{:S(2)}) async-start(), calls=%async_computation.6 | async-start | bytes 18874368 | tf_op jit(solution)/shard_map/psum | solution.py:214
  920.5 5.0 copy-start.17
  920.5 5.0 copy-start.37
  1118.4 3.4 copy-start.12
  1124.2 3.9 copy-start.1
  (27 other events, 54.0 us)
Sparse Core Ops, SparseCore 0:
  458.4 26.4 reduce-scatter.6
  488.3 26.1 reduce-scatter.8
  731.7 188.7 all-reduce.6
  923.0 195.3 all-reduce.4
